TPU v7x, 32 devices: a whole 2x2x4 slice. The times are simulated.
32 devices in a mesh: ex: 8 (over y, x, core), tp: 4 (over z).
Axes of the slice: x: 2, y: 2, z: 4, core: 2. Of those that a mesh axis runs over, the one named last changes fastest.
Arguments:
- samples: bfloat16 [192, 2048], P(('ex', 'tp')), may hold values from -6 to 6
- gate_weight: bfloat16 [2048, 44], replicated, may hold values from -15 to 15
- up_weight: bfloat16 [16, 2048, 4096], P('ex', None, 'tp'), may hold values from -0.125 to 0.125
- down_weight: bfloat16 [16, 4096, 2048], P('ex', 'tp'), may hold values from -0.09375 to 0.09375
Outputs:
- task_outputs: bfloat16 [192, 5, 2048], P(('ex', 'tp'))
All inputs are finite; a program needn't handle non-finite values.
Results may differ from a plain program's by a relative error of at most 0.0055.
Values may be sent and summed in bfloat16 or wider, within the bound.
A program may use at most 128 MiB of HBM per device.

v0:
```python
import jax
import jax.numpy as jnp
import numpy as np
from jax import lax
from jax.sharding import PartitionSpec as P

TASKS = 4
TASK_EXP = 3
SHARED = 4
EXPERTS = 16
GATES = 44


def routing_table():
    per_task = TASK_EXP + SHARED
    table = np.zeros((GATES, (TASKS + 1) * EXPERTS), np.float32)
    for task_idx in range(TASKS):
        for column in range(per_task):
            if column < TASK_EXP:
                expert_idx = task_idx * TASK_EXP + column
            else:
                expert_idx = TASKS * TASK_EXP + column - TASK_EXP
            table[task_idx * per_task + column, task_idx * EXPERTS + expert_idx] = 1.0
    for expert_idx in range(EXPERTS):
        table[TASKS * per_task + expert_idx, TASKS * EXPERTS + expert_idx] = 1.0
    return jnp.asarray(table, dtype=jnp.float32)


def gate_mix(rows, gate_weight):
    logits = jnp.dot(rows, gate_weight, preferred_element_type=jnp.float32)
    per_task = TASK_EXP + SHARED
    pieces = []
    for task_idx in range(TASKS):
        pieces.append(
            jax.nn.softmax(logits[:, task_idx * per_task : (task_idx + 1) * per_task], axis=-1)
        )
    pieces.append(jax.nn.softmax(logits[:, TASKS * per_task :], axis=-1))
    probs = jnp.concatenate(pieces, axis=1)
    mixed = jnp.dot(probs, routing_table(), precision=lax.Precision.HIGHEST)
    return mixed.reshape(rows.shape[0], TASKS + 1, EXPERTS)


def on_device(samples, gate_weight, up_weight, down_weight):
    local_experts = up_weight.shape[0]
    ex_count = lax.axis_size("ex")
    tp_count = lax.axis_size("tp")
    row_dev = samples.shape[0]
    width = samples.shape[1]
    piece = lax.all_gather(samples, ("ex", "tp"), axis=0, tiled=True)
    outputs = []
    for expert_idx in range(local_experts):
        outputs.append(
            jnp.maximum(
                jnp.dot(piece, up_weight[expert_idx], preferred_element_type=jnp.float32), 0.0
            ).astype(jnp.bfloat16)
        )
    hidden = jnp.stack(outputs, axis=1)
    partial_out = jnp.einsum(
        "rlf,lfd->rld", hidden, down_weight, preferred_element_type=jnp.float32
    )
    blocked = partial_out.reshape(ex_count, tp_count * row_dev, local_experts, width)
    summed = lax.psum_scatter(blocked, "tp", scatter_dimension=1, tiled=True)
    gathered = lax.all_to_all(summed, "ex", split_axis=0, concat_axis=2, tiled=True)[0]
    mixing = gate_mix(samples, gate_weight)
    result = jnp.einsum("rke,red->rkd", mixing, gathered, precision=lax.Precision.HIGHEST)
    return result.astype(jnp.bfloat16)


def solution(mesh):
    placed = (P(("ex", "tp"), None), P(), P("ex", None, "tp"), P("ex", "tp", None))
    return jax.shard_map(
        on_device,
        mesh=mesh,
        in_specs=placed,
        out_specs=P(("ex", "tp"), None, None),
        check_vma=False,
    )
```

profile of v0, /device:TPU:0, one launch (start us, length us, event | category | flops | bytes accessed | tf_op | source)
XLA Modules:
  0.0 185.9 jit_solution(10094937951658092538)
XLA Ops:
  6.5 0.0 copy-start
  6.5 0.0 reduce-scatter.2.cloned.1.call-start
  6.5 78.9 %all-gather = bf16[32,6,2048]{2,1,0:T(8,128)(2,1)S(1)} all-gather(bf16[1,6,2048]{2,1,0:T(8,128)(2,1)} %bitcast.43), channel_id=1, replica_groups=mesh['ex'=8,'tp'=4] {'ex','tp'}, dimensions={0}, use_global_device_ids=true | all-gather | bytes 811008 | tf_op jit(solution)/shard_map/all_gather | solution.py:49
  85.5 0.3 reshape.20
  85.7 3.2 %fusion.21 = bf16[192,1,1024]{2,0,1:T(8,128)(2,1)S(1)} fusion(bf16[192,2048]{1,0:T(8,128)(2,1)S(1)} %reshape.20, bf16[2,2048,1024]{2,1,0:T(8,128)(2,1)} %param.7), kind=kOutput, calls=%fused_computation.12 | convolution fusion | flops 805699584 | bytes 5373952 | tf_op jit(solution)/shard_map/dot_general | solution.py:54
  88.9 3.2 %fusion.18 = bf16[192,1,1024]{2,0,1:T(8,128)(2,1)S(1)} fusion(bf16[192,2048]{1,0:T(8,128)(2,1)S(1)} %reshape.20, bf16[2,2048,1024]{2,1,0:T(8,128)(2,1)} %param.7), kind=kOutput, calls=%fused_computation.11 | convolution fusion | flops 805699584 | bytes 5373952 | tf_op jit(solution)/shard_map/dot_general | solution.py:54
  92.1 5.2 %fusion.24 = f32[2,192,2048]{2,1,0:T(8,128)S(1)} fusion(bf16[2,1024,2048]{2,1,0:T(8,128)(2,1)} %param.8, bf16[192,1,1024]{2,0,1:T(8,128)(2,1)S(1)} %fusion.21, bf16[192,1,1024]{2,0,1:T(8,128)(2,1)S(1)} %fusion.18), kind=kOutput, calls=%fused_computation.17 | convolution fusion | flops 1611005952 | bytes 12320768 | tf_op jit(solution)/shard_map/rlf,lfd->rld/dot_general | solution.py:58
  97.3 0.0 copy-start.1
  97.3 0.0 copy-start.5
  97.3 0.0 copy-start.6
  97.3 0.0 copy-start.4
  97.3 0.0 copy-start.3
  97.3 0.0 copy-start.2
  97.4 3.5 %copy.10 = f32[8,24,2,2048]{3,0,2,1:T(8,128)} copy(f32[8,24,2,2048]{3,1,0,2:T(8,128)S(1)} %bitcast.41) | data formatting | bytes 6291456 | tf_op jit(solution)/shard_map/reshape | solution.py:61
  100.8 0.0 reduce-scatter.2.cloned.1.call-update
  100.9 0.0 copy-done
  100.9 0.0 copy-done.1
  100.9 0.2 fusion.50
  101.0 0.2 slice_reduce_fusion
  101.2 0.2 slice_reduce_fusion.1
  101.5 0.2 fusion.37
  101.7 0.0 copy-done.5
  101.7 0.2 fusion.31
  101.9 0.0 copy-done.6
  101.9 0.2 convolution_add_fusion.3
  102.1 56.2 %reduce-scatter.2.cloned.1.call-done = f32[8,6,2,2048]{3,0,2,1:T(8,128)} async-done(((f32[8,24,2,2048]{3,0,2,1:T(8,128)}), f32[8,6,2,2048]{3,0,2,1:T(8,128)}) %reduce-scatter.2.cloned.1.call-update) | async-done | bytes 786448 | tf_op jit(solution)/shard_map/reduce_scatter | solution.py:62
  158.3 2.6 %copy.11 = f32[8,6,2,2048]{3,2,1,0:T(2,128)} copy(f32[8,6,2,2048]{3,0,2,1:T(8,128)} %reduce-scatter.2.cloned.1.call-done) | data formatting | bytes 1572864 | tf_op jit(solution)/shard_map/reduce_scatter | solution.py:62
  161.0 3.6 %all-to-all-start = ((f32[8,6,2,2048]{3,2,1,0:T(2,128)}), f32[8,6,2,2048]{3,2,1,0:T(2,128)S(1)}, u32[]{:S(2)}, u32[]{:S(2)}) async-start(f32[8,6,2,2048]{3,2,1,0:T(2,128)} %copy.11), calls=%async_computation.1 | async-start | bytes 1572864 | tf_op jit(solution)/shard_map/all_to_all | solution.py:63
  164.6 0.2 fusion.38
  164.8 0.0 copy-done.4
  164.8 0.2 convolution_add_fusion.2
  165.0 0.0 copy-done.3
  165.0 0.2 convolution_add_fusion.1
  165.2 0.0 copy-done.2
  165.2 0.2 convolution_add_fusion
  165.4 0.1 reshape.17
  165.5 11.7 %all-to-all-done = f32[8,6,2,2048]{3,2,1,0:T(2,128)S(1)} async-done(((f32[8,6,2,2048]{3,2,1,0:T(2,128)}), f32[8,6,2,2048]{3,2,1,0:T(2,128)S(1)}, u32[]{:S(2)}, u32[]{:S(2)}) %all-to-all-start) | async-done | bytes 786464 | tf_op jit(solution)/shard_map/all_to_all | solution.py:63
  177.2 0.1 copy.12
  177.2 0.5 squeeze.11
  177.8 0.5 convolution_convert_fusion
  178.3 0.8 copy.13
Async XLA Ops:
  6.5 94.3 %copy-start = (bf16[2048,44]{0,1:T(8,128)(2,1)S(1)}, bf16[2048,44]{0,1:T(8,128)(2,1)}, u32[]{:S(2)}) copy-start(bf16[2048,44]{0,1:T(8,128)(2,1)} %param.6) | copy-start | bytes 540676
  6.5 151.8 %reduce-scatter.2.cloned.1.call-start = ((), (), s32[]{:S(2)}) async-start(), calls=%async_computation.2 | async-start | bytes 3932160 | tf_op jit(solution)/shard_map/reduce_scatter | solution.py:62
  97.3 3.6 %copy-start.1 = (bf16[6,2048]{1,0:T(8,128)(2,1)S(1)}, bf16[6,2048]{1,0:T(8,128)(2,1)}, u32[]{:S(2)}) copy-start(bf16[6,2048]{1,0:T(8,128)(2,1)} %param.5) | copy-start | bytes 73732
  97.3 4.4 %copy-start.5 = (f32[7,80]{1,0:T(8,128)S(1)}, f32[7,80]{1,0:T(8,128)}, u32[]{:S(2)}) copy-start(f32[7,80]{1,0:T(8,128)} %constant.12) | copy-start | bytes 6724
  97.3 4.6 %copy-start.6 = (f32[7,80]{1,0:T(8,128)S(1)}, f32[7,80]{1,0:T(8,128)}, u32[]{:S(2)}) copy-start(f32[7,80]{1,0:T(8,128)} %constant.13) | copy-start | bytes 6724
  97.3 67.5 %copy-start.4 = (f32[7,80]{1,0:T(8,128)S(1)}, f32[7,80]{1,0:T(8,128)}, u32[]{:S(2)}) copy-start(f32[7,80]{1,0:T(8,128)} %constant.14) | copy-start | bytes 6724
  97.3 67.7 %copy-start.3 = (f32[7,80]{1,0:T(8,128)S(1)}, f32[7,80]{1,0:T(8,128)}, u32[]{:S(2)}) copy-start(f32[7,80]{1,0:T(8,128)} %constant.15) | copy-start | bytes 6724
  97.3 67.9 %copy-start.2 = (f32[16,80]{1,0:T(8,128)S(1)}, f32[16,80]{1,0:T(8,128)}, u32[]{:S(2)}) copy-start(f32[16,80]{1,0:T(8,128)} %constant.16) | copy-start | bytes 15364
  161.0 16.2 %all-to-all-start = ((f32[8,6,2,2048]{3,2,1,0:T(2,128)}), f32[8,6,2,2048]{3,2,1,0:T(2,128)S(1)}, u32[]{:S(2)}, u32[]{:S(2)}) async-start(f32[8,6,2,2048]{3,2,1,0:T(2,128)} %copy.11), calls=%async_computation.1 | async-start | bytes 1572864 | tf_op jit(solution)/shard_map/all_to_all | solution.py:63
Sparse Core Ops, SparseCore 0:
  101.0 57.3 reduce-scatter.1
where the time goes:
time: 186 us
  blocking collectives  78.9 us (42%)
  waiting for transfers between devices  67.9 us (37%)
  between operations  13.5 us (7%)
  matrix products  13.2 us (7%)
  local copies, waits for them, and re-layouts  7.84 us (4%)
  starting transfers between devices  3.65 us (2%)
    all_gather x1, blocking collectives, on_device(): piece = lax.all_gather(samples, ('ex', 'tp'), axis=0, tiled=True)  78.9 us
    reduce_scatter x1, waiting for transfers between devices, on_device(): summed = lax.psum_scatter(blocked, 'tp', scatter_dimension=1, tiled=True)  56.2 us
    all_to_all x1, waiting for transfers between devices, on_device(): lax.all_to_all(summed, 'ex', split_axis=0, concat_axis=2, tiled=True)[0]  11.7 us
    dot_general x2, matrix products, on_device(): jnp.dot(piece, up_weight[expert_idx], preferred_element_type=jnp.float32)  6.35 us
    dot_general x1, matrix products, on_device(): jnp.einsum('rlf,lfd->rld', hidden, down_weight, preferred_element_type=jn...  5.18 us
  transfers between devices with their start and end apart: 2, of which 2 were waited for; matrix products, arithmetic and copies ran while one was open for 1% of the time, Pallas kernels for 0%

commit v1 on v0

v1 whole, which is shorter than its diff:
```python
import functools

import jax
import jax.numpy as jnp
import numpy as np
from jax import lax
from jax.experimental import pallas as pl
from jax.experimental.pallas import tpu as pltpu
from jax.sharding import PartitionSpec as P

TASKS = 4
TASK_EXP = 3
SHARED = 4
EXPERTS = 16
GATES = 44
OUTS = TASKS + 1
SLAB = 8
LANES = 128
MESH = pl.DeviceIdType.MESH


def column_facts():
    per_task = TASK_EXP + SHARED
    gate_of = np.full(LANES, -1)
    expert_of = np.full(LANES, -1)
    for column in range(TASKS * per_task):
        task_idx, j = divmod(column, per_task)
        gate_of[column] = task_idx
        expert_of[column] = (
            task_idx * TASK_EXP + j if j < TASK_EXP else TASKS * TASK_EXP + j - TASK_EXP
        )
    for expert_idx in range(EXPERTS):
        gate_of[TASKS * per_task + expert_idx] = TASKS
        expert_of[TASKS * per_task + expert_idx] = expert_idx
    return gate_of, expert_of


def constants(ex, tp, rows, experts, group):
    block = tp * rows
    out_rows = pad16(rows * OUTS)
    pack = np.zeros((group * rows, group * SLAB), np.float32)
    for slab in range(group):
        for r in range(rows):
            pack[slab * rows + r, slab * SLAB + r] = 1.0
    gate_of, expert_of = column_facts()
    total = tp * out_rows
    repeat = np.zeros((total, tp * SLAB), np.float32)
    mask = np.zeros((total, LANES), np.float32)
    column_expert = np.repeat(np.arange(ex * experts), block)
    column_row = np.tile(np.arange(block), ex * experts)
    spread = (expert_of[:, None] == column_expert[None, :]).astype(np.float32)
    match = np.zeros((total, ex * experts * block), np.float32)
    for t in range(tp):
        for q in range(out_rows):
            i = t * out_rows + q
            r, k = divmod(q, OUTS)
            if r < rows:
                repeat[i, t * SLAB + r] = 1.0
                mask[i] = gate_of == k
                match[i] = column_row == t * rows + r
            else:
                mask[i] = gate_of == TASKS
    return (
        jnp.asarray(pack, jnp.bfloat16),
        jnp.asarray(repeat, jnp.float32),
        jnp.asarray(mask, jnp.float32),
        jnp.asarray(spread, jnp.bfloat16),
        jnp.asarray(match, jnp.bfloat16),
    )


def pad16(n):
    return -(-n // 16) * 16


def kernel(
    ex, tp, chunks, group,
    x_ref, gate_ref, pack_ref, repeat_ref, mask_ref, spread_ref, match_ref, up_hbm, down_hbm,
    out_ref,
    slabs, packed, up, down, hidden, mix, send1, recv1, send2, recv2,
    up_sem, down_sem, tp_send, ex_send, sib_send, slab_recv, s1_send, s1_recv, s2_send, s2_recv,
):
    e, t = lax.axis_index("ex"), lax.axis_index("tp")
    rows, width = x_ref.shape
    experts, _, ff = up_hbm.shape
    block = tp * rows
    part = width // chunks
    half = ex // 2
    out_rows = recv2.shape[2]
    total = tp * out_rows

    up_copies = [
        pltpu.make_async_copy(up_hbm.at[l], up.at[l], up_sem.at[l]) for l in range(experts)
    ]
    down_copies = [
        pltpu.make_async_copy(down_hbm.at[l], down.at[l], down_sem.at[l]) for l in range(experts)
    ]
    for copy in up_copies + down_copies:
        copy.start()

    barrier = pltpu.get_barrier_semaphore()
    for d in range(1, tp):
        pl.semaphore_signal(
            barrier, inc=1, device_id=(e, lax.rem(t + d, tp)), device_id_type=MESH
        )
    for d in range(1, ex):
        pl.semaphore_signal(
            barrier, inc=1, device_id=(lax.rem(e + d, ex), t), device_id_type=MESH
        )
    mine = e * tp + t
    slabs[mine, :rows, :] = x_ref[...]
    slabs[mine, rows:, :] = jnp.zeros((SLAB - rows, width), jnp.bfloat16)
    pl.semaphore_wait(barrier, tp - 1 + ex - 1)

    core = lax.rem(e, 2)
    sibling = e + 1 - 2 * core

    def slab_copy(slab, send_sem, device):
        return pltpu.make_async_remote_copy(
            src_ref=slabs.at[slab],
            dst_ref=slabs.at[slab],
            send_sem=send_sem,
            recv_sem=slab_recv.at[slab],
            device_id=device,
            device_id_type=MESH,
        )

    started = []
    for d in range(1, tp):
        copy = slab_copy(mine, tp_send.at[d], (e, lax.rem(t + d, tp)))
        copy.start()
        started.append(copy)
    for step in range(tp):
        slab = e * tp + lax.rem(t + step, tp)
        if step:
            slab_copy(slab, tp_send.at[step], (e, t)).wait_recv()
        for d in range(1, half):
            copy = slab_copy(slab, ex_send.at[step, d], (lax.rem(e + 2 * d, ex), t))
            copy.start()
            started.append(copy)
        copy = slab_copy(slab, sib_send.at[0, step], (sibling, t))
        copy.start()
        started.append(copy)
    for step in range(tp):
        for d in range(1, half):
            slab = lax.rem(e + 2 * d, ex) * tp + lax.rem(t + step, tp)
            slab_copy(slab, ex_send.at[step, d], (e, t)).wait_recv()
            copy = slab_copy(slab, sib_send.at[d, step], (sibling, t))
            copy.start()
            started.append(copy)

    own = slabs[pl.ds(e * tp, tp)].astype(jnp.float32).reshape(tp * SLAB, width)
    logits = jnp.dot(
        own.astype(jnp.bfloat16), gate_ref[...], preferred_element_type=jnp.float32
    )
    logits = jnp.concatenate(
        [logits, jnp.zeros((tp * SLAB, LANES - GATES), jnp.float32)], axis=1
    )
    logits = jnp.dot(
        repeat_ref[...], logits, precision=lax.Precision.HIGHEST,
        preferred_element_type=jnp.float32,
    )
    chosen = mask_ref[...] > 0.0
    logits = jnp.where(chosen, logits, -jnp.inf)
    powers = jnp.exp(logits - jnp.max(logits, axis=1, keepdims=True))
    probs = powers / jnp.sum(powers, axis=1, keepdims=True)
    high = probs.astype(jnp.bfloat16)
    low = (probs - high.astype(jnp.float32)).astype(jnp.bfloat16)
    match = match_ref[...].astype(jnp.float32)
    for at, piece in ((0, high), (total, low)):
        placed = jnp.dot(piece, spread_ref[...], preferred_element_type=jnp.float32)
        mix[at : at + total, :] = (placed * match).astype(jnp.bfloat16)

    for step in range(tp):
        for d in range(half):
            slab = lax.rem(sibling + 2 * d, ex) * tp + lax.rem(t + step, tp)
            slab_copy(slab, sib_send.at[d, step], (e, t)).wait_recv()

    slabs_all = ex * tp
    for g in range(slabs_all // group):
        raw = slabs[g * group : (g + 1) * group].astype(jnp.float32)
        raw = raw.reshape(group * SLAB, width).astype(jnp.bfloat16)
        packed[g * group * rows : (g + 1) * group * rows, :] = jnp.dot(
            pack_ref[...], raw, preferred_element_type=jnp.float32
        ).astype(jnp.bfloat16)

    tile = min(256, ff)
    for l in range(experts):
        up_copies[l].wait()

        def up_step(i, carry, l=l):
            cols = pl.ds(pl.multiple_of(i * tile, tile), tile)
            value = jnp.dot(packed[...], up[l, :, cols], preferred_element_type=jnp.float32)
            hidden[l, :, cols] = jnp.maximum(value, 0.0).astype(jnp.bfloat16)
            return carry

        lax.fori_loop(0, ff // tile, up_step, 0)

    for copy in down_copies:
        copy.wait()

    def first_copy(c, dest, d, source_slot):
        return pltpu.make_async_remote_copy(
            src_ref=send1.at[c, dest],
            dst_ref=recv1.at[c, source_slot],
            send_sem=s1_send.at[c, d],
            recv_sem=s1_recv.at[c, source_slot],
            device_id=(dest, t),
            device_id_type=MESH,
        )

    def down_step(c, carry):
        cols = pl.ds(pl.multiple_of(c * part, part), part)
        values = [
            jnp.dot(hidden[l], down[l, :, cols], preferred_element_type=jnp.float32)
            for l in range(experts)
        ]
        for dest in range(ex):
            pieces = [v[dest * block : (dest + 1) * block] for v in values]
            joined = jnp.concatenate(pieces, axis=0) if experts > 1 else pieces[0]
            send1[c, dest] = joined.astype(jnp.bfloat16)
        for d in range(1, ex):
            first_copy(c, lax.rem(e + d, ex), d, e).start()
        recv1[c, e] = send1[c, e]
        return carry

    lax.fori_loop(0, chunks, down_step, 0)

    def second_copy(c, dest, d, source_slot):
        return pltpu.make_async_remote_copy(
            src_ref=send2.at[c, dest],
            dst_ref=recv2.at[c, source_slot],
            send_sem=s2_send.at[c, d],
            recv_sem=s2_recv.at[c, source_slot],
            device_id=(e, dest),
            device_id_type=MESH,
        )

    def mix_step(c, carry):
        for d in range(1, ex):
            first_copy(c, e, d, lax.rem(e + d, ex)).wait_recv()
        got = recv1[c].reshape(ex * experts * block, part)
        both = jnp.dot(mix[...], got, preferred_element_type=jnp.float32)
        mixed = (both[:total] + both[total:]).astype(jnp.bfloat16)
        for dest in range(tp):
            send2[c, dest] = mixed[dest * out_rows : (dest + 1) * out_rows]
        for d in range(1, tp):
            second_copy(c, lax.rem(t + d, tp), d, t).start()
        return carry

    lax.fori_loop(0, chunks, mix_step, 0)

    for c in range(chunks):
        sum_ = send2[c, t].astype(jnp.float32)
        for d in range(1, tp):
            source = lax.rem(t + d, tp)
            second_copy(c, t, d, source).wait_recv()
            sum_ = sum_ + recv2[c, source].astype(jnp.float32)
        out_ref[:, c * part : (c + 1) * part] = sum_.astype(jnp.bfloat16)

    for copy in started:
        copy.wait_send()

    def drain(c, carry):
        for d in range(1, ex):
            first_copy(c, lax.rem(e + d, ex), d, e).wait_send()
        for d in range(1, tp):
            second_copy(c, lax.rem(t + d, tp), d, t).wait_send()
        return carry

    lax.fori_loop(0, chunks, drain, 0)


def on_device(ex, tp, samples, gate_weight, up_weight, down_weight):
    experts, width, ff = up_weight.shape
    rows = samples.shape[0]
    block = tp * rows
    chunks = 4
    part = width // chunks
    group = min(32, ex * tp)
    out_rows = pad16(rows * OUTS)
    tables = constants(ex, tp, rows, experts, group)
    bf16 = jnp.bfloat16
    dma = pltpu.SemaphoreType.DMA
    vmem = pl.BlockSpec(memory_space=pltpu.VMEM)
    hbm = pl.BlockSpec(memory_space=pl.ANY)
    result = pl.pallas_call(
        functools.partial(kernel, ex, tp, chunks, group),
        out_shape=jax.ShapeDtypeStruct((out_rows, width), bf16),
        in_specs=[vmem] * 7 + [hbm] * 2,
        out_specs=vmem,
        scratch_shapes=[
            pltpu.VMEM((ex * tp, SLAB, width), bf16),
            pltpu.VMEM((ex * tp * rows, width), bf16),
            pltpu.VMEM((experts, width, ff), bf16),
            pltpu.VMEM((experts, ff, width), bf16),
            pltpu.VMEM((experts, ex * tp * rows, ff), bf16),
            pltpu.VMEM((2 * tp * out_rows, ex * experts * block), bf16),
            pltpu.VMEM((chunks, ex, experts * block, part), bf16),
            pltpu.VMEM((chunks, ex, experts * block, part), bf16),
            pltpu.VMEM((chunks, tp, out_rows, part), bf16),
            pltpu.VMEM((chunks, tp, out_rows, part), bf16),
            dma((experts,)),
            dma((experts,)),
            dma((tp,)),
            dma((tp, ex // 2)),
            dma((ex // 2, tp)),
            dma((ex * tp,)),
            dma((chunks, ex)),
            dma((chunks, ex)),
            dma((chunks, tp)),
            dma((chunks, tp)),
        ],
        compiler_params=pltpu.CompilerParams(
            collective_id=0, has_side_effects=True, vmem_limit_bytes=63_000_000
        ),
    )(samples, gate_weight, *tables, up_weight, down_weight)
    return result[: rows * OUTS].reshape(rows, OUTS, width)


def solution(mesh):
    placed = (P(("ex", "tp"), None), P(), P("ex", None, "tp"), P("ex", "tp", None))
    return jax.shard_map(
        functools.partial(on_device, mesh.shape["ex"], mesh.shape["tp"]),
        mesh=mesh,
        in_specs=placed,
        out_specs=P(("ex", "tp"), None, None),
        check_vma=False,
    )
```

time: 186 us -> 51.6 us (0.28)
  blocking collectives: 78.9 us -> 0 us
  waiting for transfers between devices: 67.9 us -> 0 us
  Pallas kernels: 0 us -> 47.7 us
  between operations: 13.5 us -> 0.01 us
  matrix products: 13.2 us -> 0 us
  local copies, waits for them, and re-layouts: 7.84 us -> 3.68 us
  starting transfers between devices: 3.65 us -> 0 us
    all_gather x1 -> x0, blocking collectives: 78.9 us -> none  [on_device(): piece = lax.all_gather(samples, ('ex', 'tp'), axis=0, tiled=True)]
    reduce_scatter x1 -> x0, waiting for transfers between devices: 56.2 us -> none  [on_device(): summed = lax.psum_scatter(blocked, 'tp', scatter_dimension=1, tiled=True)]
    pallas_call x0 -> x1, Pallas kernels: none -> 47.7 us  [on_device(): pl.pallas_call(functools.partial(kernel, ex, tp, chunks, group), out_shap...]
    dot_general x10 -> x0, matrix products: 13.2 us -> none  [the longest x2 6.35 us: on_device(): jnp.dot(piece, up_weight[expert_idx], preferred_element_type=jnp.float32)]
    all_to_all x1 -> x0, waiting for transfers between devices: 11.7 us -> none  [on_device(): lax.all_to_all(summed, 'ex', split_axis=0, concat_axis=2, tiled=True)[0]]
    all_to_all x1 -> x0, starting transfers between devices: 3.64 us -> none  [on_device(): lax.all_to_all(summed, 'ex', split_axis=0, concat_axis=2, tiled=True)[0]]
    reduce_scatter x1 -> x0, local copies, waits for them, and re-layouts: 2.62 us -> none  [on_device(): summed = lax.psum_scatter(blocked, 'tp', scatter_dimension=1, tiled=True)]
  transfers between devices with their start and end apart: 2 -> 0, of which waited for: 2 -> 0; matrix products, arithmetic and copies ran while one was open for 1% -> 0% of each run, Pallas kernels for 0% -> 0%
where the time goes in v1:
time: 51.6 us; the launch traced here: 51.4 us
  Pallas kernels  47.7 us (92%)
  local copies, waits for them, and re-layouts  3.68 us (7%)
    pallas_call x1, Pallas kernels, on_device(): pl.pallas_call(functools.partial(kernel, ex, tp, chunks, group), out_shap...  47.7 us
    unnamed x1, local copies, waits for them, and re-layouts  1.96 us
    reshape x2, local copies, waits for them, and re-layouts, on_device(): return result[:rows * OUTS].reshape(rows, OUTS, width)  1.72 us

profile of v1, /device:TPU:0, one launch (start us, length us, event | category | flops | bytes accessed | tf_op | source)
XLA Modules:
  0.0 51.4 jit_solution(1096574632833687926)
XLA Ops:
  0.0 2.0 %copy.12.gate_ref = bf16[2048,44]{1,0:T(8,128)(2,1)} copy(bf16[2048,44]{0,1:T(8,128)(2,1)} %param.10) | data formatting | bytes 360448 | tf_op args[1]
  2.0 47.7 %shard_map.91 = bf16[32,2048]{1,0:T(8,128)(2,1)} custom-call(bf16[6,2048]{1,0:T(8,128)(2,1)} %x_ref.1, bf16[2048,44]{1,0:T(8,128)(2,1)} %copy.12.gate_ref, bf16[192,256]{1,0:T(8,128)(2,1)} %constant.10.clone.pack_ref, f32[128,32]{1,0:T(8,128)} %constant.11.clone.repeat_ref, f32[128,128]{1,0:T(8,128)} %constant.12.clone.mask_ref, ...), custom_call_target="tpu_custom_call" | custom-call | tf_op jit(solution)/shard_map/pallas_call | solution.py:287
  49.7 1.0 %reshape.3 = bf16[6,5,2048]{2,1,0:T(8,128)(2,1)S(1)} reshape(bf16[30,2048]{1,0:T(8,128)(2,1)} %bitcast.1) | data formatting | bytes 245760 | tf_op jit(solution)/shard_map/reshape | solution.py:318
  50.7 0.8 %copy.13 = bf16[6,5,2048]{2,0,1:T(8,128)(2,1)} copy(bf16[6,5,2048]{2,1,0:T(8,128)(2,1)S(1)} %reshape.3) | data formatting | bytes 245760 | tf_op jit(solution)/shard_map/reshape | solution.py:318
